TPU v7x, 32 devices: a whole 2x2x4 slice. The times are simulated.
32 devices in a mesh: dp: 8 (over z, x), shard: 4 (over y, core).
Axes of the slice: x: 2, y: 2, z: 4, core: 2. Of those that a mesh axis runs over, the one named last changes fastest.
Arguments:
- tokens: bfloat16 [128, 3584], P('dp', 'shard'), may hold values from -6 to 6
- targets: bfloat16 [128, 3584], P('dp', 'shard'), may hold values from -6 to 6
- task_of_token: int32 [128], P('dp'), may hold values from 0 to 15, never falling along the last dimension, each value on 1 to 16 neighbouring positions
- up_weight: bfloat16 [18944, 3584], P('dp', 'shard'), may hold values from -0.09375 to 0.09375
- down_weight: bfloat16 [18944, 3584], P('dp', 'shard'), may hold values from -0.046875 to 0.046875
- outer_up: bfloat16 [18944, 3584], P('dp', 'shard'), may hold values from -6 to 6
- outer_down: bfloat16 [18944, 3584], P('dp', 'shard'), may hold values from -6 to 6
Outputs:
- meta_up: float32 [18944, 3584], P('dp', 'shard')
- meta_down: float32 [18944, 3584], P('dp', 'shard')
Inputs may be any that keep to these rules, and one draw needn't show every extreme that they name: `task_of_token`: task numbers never fall along the tokens; every task has 1 to 16 tokens, and some task has exactly 16.
All inputs are finite; a program needn't handle non-finite values.
Results may differ from a plain program's by a relative error of at most 0.001.
Values may be sent and summed in bfloat16 or wider, within the bound.
A program may use at most 64 MiB of HBM per device.

v0:
```python
import jax
import jax.numpy as jnp
from jax import lax
from jax.sharding import PartitionSpec as P

TASKS = 16
ITERS = 2


def sigmoid_parts(linear_part):
    argument = linear_part.astype(jnp.float32)
    logistic = jax.nn.sigmoid(argument)
    derivative = logistic * (1.0 + argument * (1.0 - logistic))
    second_order = logistic * (1.0 - logistic) * (2.0 + argument * (1.0 - 2.0 * logistic))
    return (argument * logistic, derivative, second_order)


def contract_last(left_side, right_side):
    return lax.dot_general(
        left_side, right_side, (((1,), (1,)), ((), ())), preferred_element_type=jnp.float32
    )


def contract_first(left_side, right_side):
    return lax.dot_general(
        left_side, right_side, (((0,), (0,)), ((), ())), preferred_element_type=jnp.float32
    )


def over_hidden(partial_value):
    portion = lax.psum_scatter(
        partial_value.astype(jnp.bfloat16), "shard", scatter_dimension=1, tiled=True
    )
    return lax.all_gather(portion, "shard", axis=1, tiled=True)


def over_tokens(term_fn, row_count):
    return lax.psum_scatter(
        term_fn(jnp.int32(0), row_count * lax.axis_size("dp")).astype(jnp.bfloat16),
        "dp",
        scatter_dimension=0,
        tiled=True,
    ).astype(jnp.float32)


def all_tokens(local_part):
    return lax.all_gather(local_part, "dp", axis=0, tiled=True)


def paired_sum(first_up, second_up, first_down, second_down):
    return jnp.sum(first_up * second_up) + jnp.sum(first_down * second_down)


def both_totals(residual_up, residual_down, image_up, image_down):
    return lax.psum(
        (
            paired_sum(residual_up, residual_up, residual_down, residual_down),
            paired_sum(residual_up, image_up, residual_down, image_down),
        ),
        ("dp", "shard"),
    )


def body(tokens, targets, task_of_token, up_weight, down_weight, outer_up, outer_down):
    row_count = tokens.shape[0]
    task_index = jnp.arange(TASKS, dtype=jnp.int32)
    members = (task_of_token[:, None] == task_index[None, :]).astype(jnp.float32)
    task_counts = lax.psum(jnp.sum(members, axis=0), "dp")
    inverse = 1.0 / (TASKS * task_counts)
    weight = jnp.sum(members * inverse[None, :], axis=1)
    gathered = lax.all_gather(tokens, "dp", axis=0, tiled=True)
    linear_part = over_hidden(contract_last(gathered, up_weight))
    activation, derivative, second_order = sigmoid_parts(linear_part)
    hidden = activation.astype(jnp.bfloat16)

    def forward_term(first_row, slice_rows):
        return jnp.dot(hidden, down_weight, preferred_element_type=jnp.float32)

    output_rows = over_tokens(forward_term, row_count)
    errors = (weight[:, None] * (output_rows - targets.astype(jnp.float32))).astype(jnp.bfloat16)
    all_errors = all_tokens(errors)
    backward = over_hidden(contract_last(all_errors, down_weight)).astype(jnp.float32)

    def operator(vector_up, vector_down):
        direction_up = vector_up.astype(jnp.bfloat16)
        direction_down = vector_down.astype(jnp.bfloat16)
        tangent_linear = over_hidden(contract_last(gathered, direction_up)).astype(jnp.float32)
        tangent_hidden = (derivative * tangent_linear).astype(jnp.bfloat16)

        def tangent_term(first_row, slice_rows):
            return jnp.dot(
                tangent_hidden, down_weight, preferred_element_type=jnp.float32
            ) + jnp.dot(hidden, direction_down, preferred_element_type=jnp.float32)

        tangent_output = over_tokens(tangent_term, row_count)
        tangent_errors = (weight[:, None] * tangent_output).astype(jnp.bfloat16)
        gathered_tangent = all_tokens(tangent_errors)
        tangent_backward = over_hidden(
            contract_last(gathered_tangent, down_weight) + contract_last(all_errors, direction_down)
        )
        tangent_gate = (
            derivative * tangent_backward.astype(jnp.float32)
            + second_order * backward * tangent_linear
        ).astype(jnp.bfloat16)
        hessian_up = contract_first(tangent_gate, gathered)
        hessian_down = contract_first(tangent_hidden, all_errors) + contract_first(
            hidden, gathered_tangent
        )
        return (vector_up + hessian_up, vector_down + hessian_down)

    residual_up = outer_up.astype(jnp.float32)
    residual_down = outer_down.astype(jnp.float32)
    solution_up = jnp.zeros_like(residual_up)
    solution_down = jnp.zeros_like(residual_down)
    search_up, search_down = (residual_up, residual_down)
    image_up, image_down = operator(residual_up, residual_down)
    norm_now, product = both_totals(residual_up, residual_down, image_up, image_down)
    step_size = norm_now / product
    along_up, along_down = (image_up, image_down)
    for iteration in range(ITERS):
        solution_up = solution_up + step_size * search_up
        solution_down = solution_down + step_size * search_down
        residual_up = residual_up - step_size * along_up
        residual_down = residual_down - step_size * along_down
        if iteration + 1 < ITERS:
            image_up, image_down = operator(residual_up, residual_down)
            norm_next, product = both_totals(residual_up, residual_down, image_up, image_down)
            ratio_next = norm_next / norm_now
            step_size = norm_next / (product - ratio_next * norm_next / step_size)
            search_up = residual_up + ratio_next * search_up
            search_down = residual_down + ratio_next * search_down
            along_up = image_up + ratio_next * along_up
            along_down = image_down + ratio_next * along_down
            norm_now = norm_next
    return (solution_up, solution_down)


def solution(mesh):
    placed = (
        P("dp", "shard"),
        P("dp", "shard"),
        P("dp"),
        P("dp", "shard"),
        P("dp", "shard"),
        P("dp", "shard"),
        P("dp", "shard"),
    )
    return jax.shard_map(
        body,
        mesh=mesh,
        in_specs=placed,
        out_specs=(P("dp", "shard"), P("dp", "shard")),
        check_vma=False,
    )
```

profile of v0, /device:TPU:0, one launch (start us, length us, event | category | flops | bytes accessed | tf_op | source)
XLA Modules:
  0.0 610.7 jit_solution(8272210368168391806)
XLA Ops:
  7.2 32.7 %all_gather.30 = bf16[128,896]{1,0:T(8,128)(2,1)S(1)} all-gather(bf16[16,896]{1,0:T(8,128)(2,1)} %param.7), channel_id=1, replica_groups=mesh['dp'=8,'shard'=4] {'dp'}, dimensions={0}, use_global_device_ids=true | all-gather | bytes 258048 | tf_op jit(solution)/shard_map/all_gather | solution.py:71
  39.9 4.3 convolution_convert_fusion.2
  44.3 4.3 convolution_convert_fusion.1
  48.6 18.8 %reduce-scatter.10.cloned.1.call-done = bf16[128,592]{0,1:T(8,128)(2,1)} async-done(((bf16[128,2368]{0,1:T(8,128)(2,1)}), bf16[128,592]{0,1:T(8,128)(2,1)}) %reduce-scatter.10.cloned.1.call-update) | async-done | bytes 151568 | tf_op jit(solution)/shard_map/reduce_scatter | solution.py:31
  67.5 7.2 %all_gather.31 = bf16[128,2368]{0,1:T(8,128)(2,1)S(1)} all-gather(bf16[128,592]{0,1:T(8,128)(2,1)} %reduce-scatter.10.cloned.1.call-done), channel_id=1, replica_groups=mesh['dp'=8,'shard'=4] {'shard'}, dimensions={1}, use_global_device_ids=true | all-gather | bytes 757760 | tf_op jit(solution)/shard_map/all_gather | solution.py:34
  74.7 3.9 convolution_convert_fusion.3
  78.7 14.0 %reduce-scatter.12.cloned.1.call-done = bf16[128,592]{0,1:T(8,128)(2,1)} async-done(((bf16[128,2368]{0,1:T(8,128)(2,1)}), bf16[128,592]{0,1:T(8,128)(2,1)}) %reduce-scatter.12.cloned.1.call-update) | async-done | bytes 151568 | tf_op jit(solution)/shard_map/reduce_scatter | solution.py:31
  92.8 7.4 %all_gather.32 = bf16[128,2368]{0,1:T(8,128)(2,1)S(1)} all-gather(bf16[128,592]{0,1:T(8,128)(2,1)} %reduce-scatter.12.cloned.1.call-done), channel_id=1, replica_groups=mesh['dp'=8,'shard'=4] {'shard'}, dimensions={1}, use_global_device_ids=true | all-gather | bytes 757760 | tf_op jit(solution)/shard_map/all_gather | solution.py:34
  100.1 3.4 fusion.56
  103.6 1.7 fusion.43
  105.3 0.1 convert_reduce_fusion
  105.4 21.4 %psum.36 = f32[16]{0:T(128)S(1)} all-reduce(f32[16]{0:T(128)S(1)} %convert_reduce_fusion), channel_id=1, replica_groups=mesh['dp'=8,'shard'=4] {'dp'}, use_global_device_ids=true, to_apply=%region_5.0 | all-reduce | flops 16 | bytes 128 | tf_op jit(solution)/shard_map/psum | solution.py:68
  126.8 0.2 select_reduce_fusion
  127.0 24.9 %reduce-scatter.16.cloned.1.call-done = bf16[16,896]{1,0:T(8,128)(2,1)} async-done(((bf16[128,896]{1,0:T(8,128)(2,1)}), bf16[16,896]{1,0:T(8,128)(2,1)}) %reduce-scatter.16.cloned.1.call-update) | async-done | bytes 28688 | tf_op jit(solution)/shard_map/reduce_scatter | solution.py:38
  151.8 57.9 %reduce-scatter.14.cloned.1.call-done = bf16[16,896]{1,0:T(8,128)(2,1)} async-done(((bf16[128,896]{1,0:T(8,128)(2,1)}), bf16[16,896]{1,0:T(8,128)(2,1)}) %reduce-scatter.14.cloned.1.call-update) | async-done | bytes 28688 | tf_op jit(solution)/shard_map/reduce_scatter | solution.py:38
  209.8 0.8 multiply_convert_fusion.1
  210.6 30.7 %all_gather.34 = bf16[128,896]{1,0:T(8,128)(2,1)S(1)} all-gather(bf16[16,896]{1,0:T(8,128)(2,1)S(1)} %get-tuple-element.10), channel_id=1, replica_groups=mesh['dp'=8,'shard'=4] {'dp'}, dimensions={0}, use_global_device_ids=true | all-gather | bytes 258048 | tf_op jit(solution)/shard_map/all_gather | solution.py:47
  241.3 4.3 convolution_convert_fusion
  245.7 30.7 %all_gather.33 = bf16[128,896]{1,0:T(8,128)(2,1)S(1)} all-gather(bf16[16,896]{1,0:T(8,128)(2,1)S(1)} %get-tuple-element.11), channel_id=1, replica_groups=mesh['dp'=8,'shard'=4] {'dp'}, dimensions={0}, use_global_device_ids=true | all-gather | bytes 258048 | tf_op jit(solution)/shard_map/all_gather | solution.py:47
  276.4 3.6 fusion.71
  280.1 2.1 fusion.17
  282.2 0.2 reduce-scatter.22.cloned.1.call-start
  282.4 1.4 fusion.54
  283.8 7.1 %fusion.8 = (f32[]{:T(128)}, f32[]{:T(128)}, f32[2368,896]{1,0:T(8,128)}) fusion(bf16[2368,896]{1,0:T(8,128)(2,1)} %param.13, f32[2368,896]{1,0:T(8,128)S(1)} %fusion.54, bf16[128,896]{1,0:T(8,128)(2,1)S(1)} %all_gather.33, bf16[128,2368]{0,1:T(8,128)(2,1)S(1)} %all_gather.31), kind=kOutput, calls=%fused_computation.22 | convolution fusion | flops 559833088 | bytes 22052872 | tf_op jit(solution)/shard_map/dot_general | solution.py:25
  290.9 7.8 %all_gather.36 = bf16[128,2368]{0,1:T(8,128)(2,1)S(1)} all-gather(bf16[128,592]{0,1:T(8,128)(2,1)} %reduce-scatter.20.cloned.1.call-done), channel_id=1, replica_groups=mesh['dp'=8,'shard'=4] {'shard'}, dimensions={1}, use_global_device_ids=true | all-gather | bytes 757760 | tf_op jit(solution)/shard_map/all_gather | solution.py:34
  298.7 5.0 reduce-scatter.18.cloned.1.call-done
  303.7 7.2 %all_gather.35 = bf16[128,2368]{0,1:T(8,128)(2,1)S(1)} all-gather(bf16[128,592]{0,1:T(8,128)(2,1)} %reduce-scatter.18.cloned.1.call-done), channel_id=1, replica_groups=mesh['dp'=8,'shard'=4] {'shard'}, dimensions={1}, use_global_device_ids=true | all-gather | bytes 757760 | tf_op jit(solution)/shard_map/all_gather | solution.py:34
  311.0 7.7 %fusion.3 = (f32[]{:T(128)}, f32[]{:T(128)}, f32[2368,896]{1,0:T(8,128)}) fusion(bf16[2368,896]{1,0:T(8,128)(2,1)} %param.12, bf16[128,896]{1,0:T(8,128)(2,1)S(1)} %all_gather.30, bf16[128,2368]{0,1:T(8,128)(2,1)S(1)} %all_gather.32, bf16[128,2368]{0,1:T(8,128)(2,1)S(1)} %all_gather.35, bf16[128,2368]{0,1:T(8,128)(2,1)S(1)} %all_gather.36, ...), kind=kOutput, calls=%fused_computation.17 | convolution fusion | flops 562561024 | bytes 15384584 | tf_op jit(solution)/shard_map/dot_general | solution.py:25
  321.2 39.9 %all-reduce.1 = (f32[]{:T(128)}, f32[]{:T(128)}) all-reduce(f32[]{:T(128)S(6)} %add.97, f32[]{:T(128)S(6)} %add.107), channel_id=1, replica_groups=mesh['dp'=8,'shard'=4] {'dp','shard'}, use_global_device_ids=true, to_apply=%region_2.0 | all-reduce | flops 2 | bytes 16 | tf_op jit(solution)/shard_map/psum | solution.py:55
  362.3 7.0 %fusion.19 = bf16[128,2368]{0,1:T(8,128)(2,1)} fusion(bf16[128,896]{1,0:T(8,128)(2,1)S(1)} %all_gather.30, bf16[2368,896]{1,0:T(8,128)(2,1)} %param.12, f32[2368,896]{1,0:T(8,128)} %get-tuple-element.12, f32[]{:T(128)S(6)} %div.20), kind=kOutput, calls=%fused_computation.38 | convolution fusion | flops 554074112 | bytes 13565956 | tf_op jit(solution)/shard_map/dot_general | solution.py:19
  369.4 7.4 %multiply_reduce_fusion.1 = f32[]{:T(128)} fusion(f32[2368,896]{1,0:T(8,128)} %get-tuple-element.12, f32[]{:T(128)S(6)} %div.20, bf16[2368,896]{1,0:T(8,128)(2,1)} %param.12), kind=kLoop, calls=%fused_computation.27 | loop fusion | flops 12730367 | bytes 12730376 | tf_op jit(solution)/shard_map/reduce_sum | solution.py:51
  376.7 15.2 %reduce-scatter.22.cloned.1.call-done = bf16[128,592]{0,1:T(8,128)(2,1)} async-done(((bf16[128,2368]{0,1:T(8,128)(2,1)}), bf16[128,592]{0,1:T(8,128)(2,1)}) %reduce-scatter.22.cloned.1.call-update) | async-done | bytes 151568 | tf_op jit(solution)/shard_map/reduce_scatter | solution.py:31
  392.0 7.5 %all_gather.37 = bf16[128,2368]{0,1:T(8,128)(2,1)S(1)} all-gather(bf16[128,592]{0,1:T(8,128)(2,1)} %reduce-scatter.22.cloned.1.call-done), channel_id=1, replica_groups=mesh['dp'=8,'shard'=4] {'shard'}, dimensions={1}, use_global_device_ids=true | all-gather | bytes 757760 | tf_op jit(solution)/shard_map/all_gather | solution.py:34
  399.4 3.4 fusion.52
  402.8 7.1 %fusion.44 = bf16[128,896]{1,0:T(8,128)(2,1)} fusion(f32[128,896]{1,0:T(8,128)S(1)} %fusion.52, bf16[2368,896]{1,0:T(8,128)(2,1)} %param.13, f32[2368,896]{1,0:T(8,128)} %get-tuple-element.13, f32[]{:T(128)S(6)} %div.20, bf16[128,2368]{0,1:T(8,128)(2,1)S(1)} %all_gather.31), kind=kOutput, calls=%fused_computation.69 | convolution fusion | flops 553697280 | bytes 14024708 | tf_op jit(solution)/shard_map/dot_general | solution.py:93
  410.0 7.5 %multiply_reduce_fusion = f32[]{:T(128)} fusion(f32[2368,896]{1,0:T(8,128)} %get-tuple-element.13, f32[]{:T(128)S(6)} %div.20, bf16[2368,896]{1,0:T(8,128)(2,1)} %param.13), kind=kLoop, calls=%fused_computation.26 | loop fusion | flops 10608639 | bytes 12730376 | tf_op jit(solution)/shard_map/reduce_sum | solution.py:51
  418.6 47.3 %reduce-scatter.24.cloned.1.call-done = bf16[16,896]{1,0:T(8,128)(2,1)} async-done(((bf16[128,896]{1,0:T(8,128)(2,1)}), bf16[16,896]{1,0:T(8,128)(2,1)}) %reduce-scatter.24.cloned.1.call-update) | async-done | bytes 28688 | tf_op jit(solution)/shard_map/reduce_scatter | solution.py:38
  465.9 0.8 multiply_convert_fusion
  466.7 30.7 %all_gather.38 = bf16[128,896]{1,0:T(8,128)(2,1)S(1)} all-gather(bf16[16,896]{1,0:T(8,128)(2,1)S(1)} %multiply_convert_fusion), channel_id=1, replica_groups=mesh['dp'=8,'shard'=4] {'dp'}, dimensions={0}, use_global_device_ids=true | all-gather | bytes 258048 | tf_op jit(solution)/shard_map/all_gather | solution.py:47
  497.5 3.5 fusion.72
  500.9 6.9 %fusion.18 = bf16[128,2368]{0,1:T(8,128)(2,1)} fusion(f32[128,2368]{0,1:T(8,128)S(1)} %fusion.72, bf16[128,896]{1,0:T(8,128)(2,1)S(1)} %all_gather.34, bf16[2368,896]{1,0:T(8,128)(2,1)} %param.13, f32[2368,896]{1,0:T(8,128)} %get-tuple-element.13, f32[]{:T(128)S(6)} %div.20), kind=kOutput, calls=%fused_computation.37 | convolution fusion | flops 552255488 | bytes 14778372 | tf_op jit(solution)/shard_map/dot_general | solution.py:19
  507.8 1.4 fusion.50
  509.2 6.7 %fusion.1 = f32[]{:T(128)} fusion(f32[2368,896]{1,0:T(8,128)S(1)} %fusion.50, bf16[128,896]{1,0:T(8,128)(2,1)S(1)} %all_gather.38, f32[2368,896]{1,0:T(8,128)} %get-tuple-element.13, f32[]{:T(128)S(6)} %div.20, bf16[2368,896]{1,0:T(8,128)(2,1)} %param.13, bf16[128,2368]{0,1:T(8,128)(2,1)S(1)} %all_gather.31), kind=kOutput, calls=%fused_computation.15 | convolution fusion | flops 559833088 | bytes 22052872 | tf_op jit(solution)/shard_map/dot_general | solution.py:25
  515.9 13.5 %reduce-scatter.26.cloned.1.call-done = bf16[128,592]{0,1:T(8,128)(2,1)} async-done(((bf16[128,2368]{0,1:T(8,128)(2,1)}), bf16[128,592]{0,1:T(8,128)(2,1)}) %reduce-scatter.26.cloned.1.call-update) | async-done | bytes 151568 | tf_op jit(solution)/shard_map/reduce_scatter | solution.py:31
  529.3 7.5 %all_gather.39 = bf16[128,2368]{0,1:T(8,128)(2,1)S(1)} all-gather(bf16[128,592]{0,1:T(8,128)(2,1)} %reduce-scatter.26.cloned.1.call-done), channel_id=1, replica_groups=mesh['dp'=8,'shard'=4] {'shard'}, dimensions={1}, use_global_device_ids=true | all-gather | bytes 757760 | tf_op jit(solution)/shard_map/all_gather | solution.py:34
  536.8 7.0 %fusion = f32[]{:T(128)} fusion(bf16[128,896]{1,0:T(8,128)(2,1)S(1)} %all_gather.30, bf16[128,2368]{0,1:T(8,128)(2,1)S(1)} %all_gather.37, bf16[128,2368]{0,1:T(8,128)(2,1)S(1)} %all_gather.39, f32[2368,896]{1,0:T(8,128)} %get-tuple-element.12, f32[]{:T(128)S(6)} %div.20, bf16[2368,896]{1,0:T(8,128)(2,1)} %param.12, bf16[128,2368]{0,1:T(8,128)(2,1)S(1)} %all_gather.31, ...), kind=kOutput, calls=%fused_computation.14 | convolution fusion | flops 564682752 | bytes 15384584 | tf_op jit(solution)/shard_map/dot_general | solution.py:25
  545.0 39.9 %all-reduce = (f32[]{:T(128)}, f32[]{:T(128)}) all-reduce(f32[]{:T(128)S(6)} %add.108, f32[]{:T(128)S(6)} %add.115), channel_id=1, replica_groups=mesh['dp'=8,'shard'=4] {'dp','shard'}, use_global_device_ids=true, to_apply=%region_17.0 | all-reduce | flops 2 | bytes 16 | tf_op jit(solution)/shard_map/psum | solution.py:55
  589.3 14.8 %fusion.4 = (f32[2368,896]{1,0:T(8,128)}, f32[2368,896]{1,0:T(8,128)}) fusion(bf16[2368,896]{1,0:T(8,128)(2,1)} %param.12, f32[]{:T(128)S(6)} %div.21, f32[]{:T(128)S(6)} %div.23, f32[]{:T(128)S(6)} %div.20, f32[2368,896]{1,0:T(8,128)} %get-tuple-element.12, f32[2368,896]{1,0:T(8,128)} %get-tuple-element.13, bf16[2368,896]{1,0:T(8,128)(2,1)} %param.13), kind=kLoop, calls=%fused_computation.18 | loop fusion | flops 36069376 | bytes 42434572 | tf_op jit(solution)/shard_map/add | solution.py:121
  (33 shorter events, 0.5 us)
Async XLA Ops:
  7.2 60.3 %reduce-scatter.10.cloned.1.call-start = ((), (), s32[]{:S(2)}) async-start(), calls=%async_computation.9 | async-start | bytes 757760 | tf_op jit(solution)/shard_map/reduce_scatter | solution.py:31
  44.2 48.5 %reduce-scatter.12.cloned.1.call-start = ((), (), s32[]{:S(2)}) async-start(), calls=%async_computation.10 | async-start | bytes 757760 | tf_op jit(solution)/shard_map/reduce_scatter | solution.py:31
  48.6 103.2 %reduce-scatter.16.cloned.1.call-start = ((), (), s32[]{:S(2)}) async-start(), calls=%async_computation.12 | async-start | bytes 258048 | tf_op jit(solution)/shard_map/reduce_scatter | solution.py:38
  78.7 131.1 %reduce-scatter.14.cloned.1.call-start = ((), (), s32[]{:S(2)}) async-start(), calls=%async_computation.11 | async-start | bytes 258048 | tf_op jit(solution)/shard_map/reduce_scatter | solution.py:38
  92.8 10.8 %slice-start = ((s8[4243456]{0:T(1024)(128)(4,1)}), s8[4194304]{0:T(1024)(128)(4,1)S(1)}, s32[]{:S(2)}) async-start(s8[4243456]{0:T(1024)(128)(4,1)} %bitcast.26), calls=%async_computation.18 | async-start | bytes 8388608
  100.1 3.4 slice-start.1
  103.5 1.8 copy-start.1
  103.5 106.2 %copy-start = (bf16[16,896]{1,0:T(8,128)(2,1)S(1)}, bf16[16,896]{1,0:T(8,128)(2,1)}, u32[]{:S(2)}) copy-start(bf16[16,896]{1,0:T(8,128)(2,1)} %param.8) | copy-start | bytes 86020
  105.2 185.7 %reduce-scatter.20.cloned.1.call-start = ((), (), s32[]{:S(2)}) async-start(), calls=%async_computation.14 | async-start | bytes 757760 | tf_op jit(solution)/shard_map/reduce_scatter | solution.py:31
  245.6 34.4 %slice-start.2 = ((s8[4243456]{0:T(1024)(128)(4,1)}), s8[49152]{0:T(1024)(128)(4,1)S(1)}, s32[]{:S(2)}) async-start(s8[4243456]{0:T(1024)(128)(4,1)} %bitcast.28), calls=%async_computation.20 | async-start | bytes 98304
  245.7 58.1 %reduce-scatter.18.cloned.1.call-start = ((), (), s32[]{:S(2)}) async-start(), calls=%async_computation.13 | async-start | bytes 757760 | tf_op jit(solution)/shard_map/reduce_scatter | solution.py:31
  276.4 3.7 slice-start.3
  282.2 109.8 %reduce-scatter.22.cloned.1.call-start = ((), (), s32[]{:S(2)}) async-start(), calls=%async_computation.15 | async-start | bytes 757760 | tf_op jit(solution)/shard_map/reduce_scatter | solution.py:31
  369.3 96.6 %reduce-scatter.24.cloned.1.call-start = ((), (), s32[]{:S(2)}) async-start(), calls=%async_computation.16 | async-start | bytes 258048 | tf_op jit(solution)/shard_map/reduce_scatter | solution.py:38
  409.9 119.4 %reduce-scatter.26.cloned.1.call-start = ((), (), s32[]{:S(2)}) async-start(), calls=%async_computation.17 | async-start | bytes 757760 | tf_op jit(solution)/shard_map/reduce_scatter | solution.py:31
Sparse Core Ops, SparseCore 0:
  44.4 23.0 reduce-scatter.9
  70.6 22.1 reduce-scatter.11
  96.5 55.2 reduce-scatter.15
  155.4 54.3 reduce-scatter.13
  245.8 21.3 reduce-scatter.19
  282.3 21.3 reduce-scatter.17
  369.4 22.5 reduce-scatter.21
  410.1 55.8 reduce-scatter.23
  508.0 21.3 reduce-scatter.25
where the time goes:
time: 612 us; the launch traced here: 611 us
  blocking collectives  271 us (44%)
  waiting for transfers between devices  197 us (32%)
  matrix products  86.5 us (14%)
  other arithmetic  31.6 us (5%)
  between operations  24.6 us (4%)
    reduce_scatter x3, waiting for transfers between devices, over_tokens(): lax.psum_scatter(term_fn(jnp.int32(0), row_count * lax.axis_size('dp')).a...  130 us
    all_gather x3, blocking collectives, all_tokens(): return lax.all_gather(local_part, 'dp', axis=0, tiled=True)  92.1 us
    psum x2, blocking collectives, both_totals(): lax.psum((paired_sum(residual_up, residual_up, residual_down, residual_do...  79.7 us
    reduce_scatter x6, waiting for transfers between devices, over_hidden(): lax.psum_scatter(partial_value.astype(jnp.bfloat16), 'shard', scatter_dim...  66.6 us
    all_gather x6, blocking collectives, over_hidden(): return lax.all_gather(portion, 'shard', axis=1, tiled=True)  44.6 us
    dot_general x8, matrix products, contract_last(): lax.dot_general(left_side, right_side, (((1,), (1,)), ((), ())), preferre...  35.9 us
    all_gather x1, blocking collectives, body(): gathered = lax.all_gather(tokens, 'dp', axis=0, tiled=True)  32.7 us
    dot_general x6, matrix products, contract_first(): lax.dot_general(left_side, right_side, (((0,), (0,)), ((), ())), preferre...  31.2 us
  transfers between devices with their start and end apart: 9, of which 8 were waited for; matrix products, arithmetic and copies ran while one was open for 8% of the time, Pallas kernels for 0%

commit v1 on v0

--- a/solution.py
+++ b/solution.py
@@ -53,11 +53,14 @@
 
 def both_totals(residual_up, residual_down, image_up, image_down):
     return lax.psum(
-        (
-            paired_sum(residual_up, residual_up, residual_down, residual_down),
-            paired_sum(residual_up, image_up, residual_down, image_down),
+        lax.psum(
+            (
+                paired_sum(residual_up, residual_up, residual_down, residual_down),
+                paired_sum(residual_up, image_up, residual_down, image_down),
+            ),
+            "shard",
         ),
-        ("dp", "shard"),
+        "dp",
     )
 
 

time: 612 us -> 587 us (0.959)
  blocking collectives: 271 us -> 249 us
    psum x2, blocking collectives: 79.7 us -> 14.6 us  [both_totals(): lax.psum((paired_sum(residual_up, residual_up, residual_down, residual_do...]
    psum x0 -> x2, blocking collectives: none -> 44.3 us  [both_totals(): lax.psum(lax.psum((paired_sum(residual_up, residual_up, residual_down, re...]
  transfers between devices with their start and end apart: 9 -> 9, of which waited for: 8 -> 8; matrix products, arithmetic and copies ran while one was open for 8% -> 9% of each run, Pallas kernels for 0% -> 0%
where the time goes in v1:
time: 587 us; the launch traced here: 586 us
  blocking collectives  249 us (42%)
  waiting for transfers between devices  193 us (33%)
  matrix products  86.5 us (15%)
  other arithmetic  31.8 us (5%)
  between operations  24.6 us (4%)
    reduce_scatter x3, waiting for transfers between devices, over_tokens(): lax.psum_scatter(term_fn(jnp.int32(0), row_count * lax.axis_size('dp')).a...  130 us
    all_gather x3, blocking collectives, all_tokens(): return lax.all_gather(local_part, 'dp', axis=0, tiled=True)  92.1 us
    reduce_scatter x6, waiting for transfers between devices, over_hidden(): lax.psum_scatter(partial_value.astype(jnp.bfloat16), 'shard', scatter_dim...  62.7 us
    psum x2, blocking collectives, both_totals(): lax.psum(lax.psum((paired_sum(residual_up, residual_up, residual_down, re...  44.3 us
    all_gather x6, blocking collectives, over_hidden(): return lax.all_gather(portion, 'shard', axis=1, tiled=True)  44.1 us
    dot_general x8, matrix products, contract_last(): lax.dot_general(left_side, right_side, (((1,), (1,)), ((), ())), preferre...  35.9 us
    all_gather x1, blocking collectives, body(): gathered = lax.all_gather(tokens, 'dp', axis=0, tiled=True)  32.7 us
    dot_general x6, matrix products, contract_first(): lax.dot_general(left_side, right_side, (((0,), (0,)), ((), ())), preferre...  31.2 us
  transfers between devices with their start and end apart: 9, of which 8 were waited for; matrix products, arithmetic and copies ran while one was open for 9% of the time, Pallas kernels for 0%

profile of v1, /device:TPU:0, one launch (start us, length us, event | category | flops | bytes accessed | tf_op | source)
XLA Modules:
  0.0 585.7 jit_solution(6819534795907611993)
XLA Ops:
  7.2 32.7 %all_gather.30 = bf16[128,896]{1,0:T(8,128)(2,1)S(1)} all-gather(bf16[16,896]{1,0:T(8,128)(2,1)} %param.7), channel_id=1, replica_groups=mesh['dp'=8,'shard'=4] {'dp'}, dimensions={0}, use_global_device_ids=true | all-gather | bytes 258048 | tf_op jit(solution)/shard_map/all_gather | solution.py:74
  39.9 4.3 convolution_convert_fusion.2
  44.3 4.3 convolution_convert_fusion.1
  48.6 18.8 %reduce-scatter.10.cloned.1.call-done = bf16[128,592]{0,1:T(8,128)(2,1)} async-done(((bf16[128,2368]{0,1:T(8,128)(2,1)}), bf16[128,592]{0,1:T(8,128)(2,1)}) %reduce-scatter.10.cloned.1.call-update) | async-done | bytes 151568 | tf_op jit(solution)/shard_map/reduce_scatter | solution.py:31
  67.5 7.2 %all_gather.31 = bf16[128,2368]{0,1:T(8,128)(2,1)S(1)} all-gather(bf16[128,592]{0,1:T(8,128)(2,1)} %reduce-scatter.10.cloned.1.call-done), channel_id=1, replica_groups=mesh['dp'=8,'shard'=4] {'shard'}, dimensions={1}, use_global_device_ids=true | all-gather | bytes 757760 | tf_op jit(solution)/shard_map/all_gather | solution.py:34
  74.7 3.9 convolution_convert_fusion.3
  78.7 14.0 %reduce-scatter.12.cloned.1.call-done = bf16[128,592]{0,1:T(8,128)(2,1)} async-done(((bf16[128,2368]{0,1:T(8,128)(2,1)}), bf16[128,592]{0,1:T(8,128)(2,1)}) %reduce-scatter.12.cloned.1.call-update) | async-done | bytes 151568 | tf_op jit(solution)/shard_map/reduce_scatter | solution.py:31
  92.8 7.4 %all_gather.32 = bf16[128,2368]{0,1:T(8,128)(2,1)S(1)} all-gather(bf16[128,592]{0,1:T(8,128)(2,1)} %reduce-scatter.12.cloned.1.call-done), channel_id=1, replica_groups=mesh['dp'=8,'shard'=4] {'shard'}, dimensions={1}, use_global_device_ids=true | all-gather | bytes 757760 | tf_op jit(solution)/shard_map/all_gather | solution.py:34
  100.1 3.4 fusion.56
  103.6 1.7 fusion.43
  105.4 21.4 %psum.65 = f32[16]{0:T(128)S(1)} all-reduce(f32[16]{0:T(128)S(1)} %convert_reduce_fusion), channel_id=1, replica_groups=mesh['dp'=8,'shard'=4] {'dp'}, use_global_device_ids=true, to_apply=%region_6.0 | all-reduce | flops 16 | bytes 128 | tf_op jit(solution)/shard_map/psum | solution.py:71
  127.0 24.9 %reduce-scatter.16.cloned.1.call-done = bf16[16,896]{1,0:T(8,128)(2,1)} async-done(((bf16[128,896]{1,0:T(8,128)(2,1)}), bf16[16,896]{1,0:T(8,128)(2,1)}) %reduce-scatter.16.cloned.1.call-update) | async-done | bytes 28688 | tf_op jit(solution)/shard_map/reduce_scatter | solution.py:38
  151.8 57.9 %reduce-scatter.14.cloned.1.call-done = bf16[16,896]{1,0:T(8,128)(2,1)} async-done(((bf16[128,896]{1,0:T(8,128)(2,1)}), bf16[16,896]{1,0:T(8,128)(2,1)}) %reduce-scatter.14.cloned.1.call-update) | async-done | bytes 28688 | tf_op jit(solution)/shard_map/reduce_scatter | solution.py:38
  209.8 0.8 multiply_convert_fusion.1
  210.6 30.7 %all_gather.34 = bf16[128,896]{1,0:T(8,128)(2,1)S(1)} all-gather(bf16[16,896]{1,0:T(8,128)(2,1)S(1)} %get-tuple-element.14), channel_id=1, replica_groups=mesh['dp'=8,'shard'=4] {'dp'}, dimensions={0}, use_global_device_ids=true | all-gather | bytes 258048 | tf_op jit(solution)/shard_map/all_gather | solution.py:47
  241.3 4.3 convolution_convert_fusion
  245.7 30.7 %all_gather.33 = bf16[128,896]{1,0:T(8,128)(2,1)S(1)} all-gather(bf16[16,896]{1,0:T(8,128)(2,1)S(1)} %get-tuple-element.15), channel_id=1, replica_groups=mesh['dp'=8,'shard'=4] {'dp'}, dimensions={0}, use_global_device_ids=true | all-gather | bytes 258048 | tf_op jit(solution)/shard_map/all_gather | solution.py:47
  276.4 3.6 fusion.71
  280.1 2.1 fusion.17
  282.4 1.4 fusion.54
  283.8 7.1 %fusion.8 = (f32[]{:T(128)}, f32[]{:T(128)}, f32[2368,896]{1,0:T(8,128)}) fusion(bf16[2368,896]{1,0:T(8,128)(2,1)} %param.13, f32[2368,896]{1,0:T(8,128)S(1)} %fusion.54, bf16[128,896]{1,0:T(8,128)(2,1)S(1)} %all_gather.33, bf16[128,2368]{0,1:T(8,128)(2,1)S(1)} %all_gather.31), kind=kOutput, calls=%fused_computation.22 | convolution fusion | flops 559833088 | bytes 22052872 | tf_op jit(solution)/shard_map/dot_general | solution.py:25
  290.9 7.8 %all_gather.36 = bf16[128,2368]{0,1:T(8,128)(2,1)S(1)} all-gather(bf16[128,592]{0,1:T(8,128)(2,1)} %reduce-scatter.20.cloned.1.call-done), channel_id=1, replica_groups=mesh['dp'=8,'shard'=4] {'shard'}, dimensions={1}, use_global_device_ids=true | all-gather | bytes 757760 | tf_op jit(solution)/shard_map/all_gather | solution.py:34
  298.7 5.0 reduce-scatter.18.cloned.1.call-done
  303.7 7.2 %all_gather.35 = bf16[128,2368]{0,1:T(8,128)(2,1)S(1)} all-gather(bf16[128,592]{0,1:T(8,128)(2,1)} %reduce-scatter.18.cloned.1.call-done), channel_id=1, replica_groups=mesh['dp'=8,'shard'=4] {'shard'}, dimensions={1}, use_global_device_ids=true | all-gather | bytes 757760 | tf_op jit(solution)/shard_map/all_gather | solution.py:34
  311.0 7.7 %fusion.3 = (f32[]{:T(128)}, f32[]{:T(128)}, f32[2368,896]{1,0:T(8,128)}) fusion(bf16[2368,896]{1,0:T(8,128)(2,1)} %param.12, bf16[128,896]{1,0:T(8,128)(2,1)S(1)} %all_gather.30, bf16[128,2368]{0,1:T(8,128)(2,1)S(1)} %all_gather.32, bf16[128,2368]{0,1:T(8,128)(2,1)S(1)} %all_gather.35, bf16[128,2368]{0,1:T(8,128)(2,1)S(1)} %all_gather.36, ...), kind=kOutput, calls=%fused_computation.17 | convolution fusion | flops 562561024 | bytes 15384584 | tf_op jit(solution)/shard_map/dot_general | solution.py:25
  321.2 7.3 %all-reduce.3 = (f32[]{:T(128)}, f32[]{:T(128)}) all-reduce(f32[]{:T(128)S(6)} %add.105, f32[]{:T(128)S(6)} %add.115), channel_id=1, replica_groups=mesh['dp'=8,'shard'=4] {'shard'}, use_global_device_ids=true, to_apply=%region_2.0 | all-reduce | flops 2 | bytes 16 | tf_op jit(solution)/shard_map/psum | solution.py:56
  328.5 22.0 %all-reduce.1 = (f32[]{:T(128)}, f32[]{:T(128)}) all-reduce(f32[]{:T(128)} %get-tuple-element.12, f32[]{:T(128)} %get-tuple-element.13), channel_id=1, replica_groups=mesh['dp'=8,'shard'=4] {'dp'}, use_global_device_ids=true, to_apply=%region_3.0 | all-reduce | flops 2 | bytes 16 | tf_op jit(solution)/shard_map/psum | solution.py:55
  351.8 7.0 %fusion.19 = bf16[128,2368]{0,1:T(8,128)(2,1)} fusion(bf16[128,896]{1,0:T(8,128)(2,1)S(1)} %all_gather.30, bf16[2368,896]{1,0:T(8,128)(2,1)} %param.12, f32[2368,896]{1,0:T(8,128)} %get-tuple-element.16, f32[]{:T(128)S(6)} %div.20), kind=kOutput, calls=%fused_computation.38 | convolution fusion | flops 554074112 | bytes 13565956 | tf_op jit(solution)/shard_map/dot_general | solution.py:19
  358.8 7.6 %multiply_reduce_fusion.1 = f32[]{:T(128)} fusion(f32[2368,896]{1,0:T(8,128)} %get-tuple-element.16, f32[]{:T(128)S(6)} %div.20, bf16[2368,896]{1,0:T(8,128)(2,1)} %param.12), kind=kLoop, calls=%fused_computation.27 | loop fusion | flops 12730367 | bytes 12730376 | tf_op jit(solution)/shard_map/reduce_sum | solution.py:51
  366.5 11.3 %reduce-scatter.22.cloned.1.call-done = bf16[128,592]{0,1:T(8,128)(2,1)} async-done(((bf16[128,2368]{0,1:T(8,128)(2,1)}), bf16[128,592]{0,1:T(8,128)(2,1)}) %reduce-scatter.22.cloned.1.call-update) | async-done | bytes 151568 | tf_op jit(solution)/shard_map/reduce_scatter | solution.py:31
  377.8 7.2 %all_gather.37 = bf16[128,2368]{0,1:T(8,128)(2,1)S(1)} all-gather(bf16[128,592]{0,1:T(8,128)(2,1)} %reduce-scatter.22.cloned.1.call-done), channel_id=1, replica_groups=mesh['dp'=8,'shard'=4] {'shard'}, dimensions={1}, use_global_device_ids=true | all-gather | bytes 757760 | tf_op jit(solution)/shard_map/all_gather | solution.py:34
  385.0 3.4 fusion.52
  388.4 7.1 %fusion.44 = bf16[128,896]{1,0:T(8,128)(2,1)} fusion(f32[128,896]{1,0:T(8,128)S(1)} %fusion.52, bf16[2368,896]{1,0:T(8,128)(2,1)} %param.13, f32[2368,896]{1,0:T(8,128)} %get-tuple-element.17, f32[]{:T(128)S(6)} %div.20, bf16[128,2368]{0,1:T(8,128)(2,1)S(1)} %all_gather.31), kind=kOutput, calls=%fused_computation.69 | convolution fusion | flops 553697280 | bytes 14024708 | tf_op jit(solution)/shard_map/dot_general | solution.py:96
  395.5 0.3 reduce-scatter.26.cloned.1.call-start
  395.8 7.5 %multiply_reduce_fusion = f32[]{:T(128)} fusion(f32[2368,896]{1,0:T(8,128)} %get-tuple-element.17, f32[]{:T(128)S(6)} %div.20, bf16[2368,896]{1,0:T(8,128)(2,1)} %param.13), kind=kLoop, calls=%fused_computation.26 | loop fusion | flops 10608639 | bytes 12730376 | tf_op jit(solution)/shard_map/reduce_sum | solution.py:51
  404.4 47.1 %reduce-scatter.24.cloned.1.call-done = bf16[16,896]{1,0:T(8,128)(2,1)} async-done(((bf16[128,896]{1,0:T(8,128)(2,1)}), bf16[16,896]{1,0:T(8,128)(2,1)}) %reduce-scatter.24.cloned.1.call-update) | async-done | bytes 28688 | tf_op jit(solution)/shard_map/reduce_scatter | solution.py:38
  451.5 0.8 multiply_convert_fusion
  452.4 30.7 %all_gather.38 = bf16[128,896]{1,0:T(8,128)(2,1)S(1)} all-gather(bf16[16,896]{1,0:T(8,128)(2,1)S(1)} %multiply_convert_fusion), channel_id=1, replica_groups=mesh['dp'=8,'shard'=4] {'dp'}, dimensions={0}, use_global_device_ids=true | all-gather | bytes 258048 | tf_op jit(solution)/shard_map/all_gather | solution.py:47
  483.0 3.5 fusion.72
  486.5 6.9 %fusion.18 = bf16[128,2368]{0,1:T(8,128)(2,1)} fusion(f32[128,2368]{0,1:T(8,128)S(1)} %fusion.72, bf16[128,896]{1,0:T(8,128)(2,1)S(1)} %all_gather.34, bf16[2368,896]{1,0:T(8,128)(2,1)} %param.13, f32[2368,896]{1,0:T(8,128)} %get-tuple-element.17, f32[]{:T(128)S(6)} %div.20), kind=kOutput, calls=%fused_computation.37 | convolution fusion | flops 552255488 | bytes 14778372 | tf_op jit(solution)/shard_map/dot_general | solution.py:19
  493.4 1.4 fusion.50
  494.8 6.7 %fusion.1 = f32[]{:T(128)} fusion(f32[2368,896]{1,0:T(8,128)S(1)} %fusion.50, bf16[128,896]{1,0:T(8,128)(2,1)S(1)} %all_gather.38, f32[2368,896]{1,0:T(8,128)} %get-tuple-element.17, f32[]{:T(128)S(6)} %div.20, bf16[2368,896]{1,0:T(8,128)(2,1)} %param.13, bf16[128,2368]{0,1:T(8,128)(2,1)S(1)} %all_gather.31), kind=kOutput, calls=%fused_computation.15 | convolution fusion | flops 559833088 | bytes 22052872 | tf_op jit(solution)/shard_map/dot_general | solution.py:25
  501.5 13.5 %reduce-scatter.26.cloned.1.call-done = bf16[128,592]{0,1:T(8,128)(2,1)} async-done(((bf16[128,2368]{0,1:T(8,128)(2,1)}), bf16[128,592]{0,1:T(8,128)(2,1)}) %reduce-scatter.26.cloned.1.call-update) | async-done | bytes 151568 | tf_op jit(solution)/shard_map/reduce_scatter | solution.py:31
  514.9 7.2 %all_gather.39 = bf16[128,2368]{0,1:T(8,128)(2,1)S(1)} all-gather(bf16[128,592]{0,1:T(8,128)(2,1)} %reduce-scatter.26.cloned.1.call-done), channel_id=1, replica_groups=mesh['dp'=8,'shard'=4] {'shard'}, dimensions={1}, use_global_device_ids=true | all-gather | bytes 757760 | tf_op jit(solution)/shard_map/all_gather | solution.py:34
  522.2 7.0 %fusion = f32[]{:T(128)} fusion(bf16[128,896]{1,0:T(8,128)(2,1)S(1)} %all_gather.30, bf16[128,2368]{0,1:T(8,128)(2,1)S(1)} %all_gather.37, bf16[128,2368]{0,1:T(8,128)(2,1)S(1)} %all_gather.39, f32[2368,896]{1,0:T(8,128)} %get-tuple-element.16, f32[]{:T(128)S(6)} %div.20, bf16[2368,896]{1,0:T(8,128)(2,1)} %param.12, bf16[128,2368]{0,1:T(8,128)(2,1)S(1)} %all_gather.31, ...), kind=kOutput, calls=%fused_computation.14 | convolution fusion | flops 564682752 | bytes 15384584 | tf_op jit(solution)/shard_map/dot_general | solution.py:25
  530.4 7.3 %all-reduce.2 = (f32[]{:T(128)}, f32[]{:T(128)}) all-reduce(f32[]{:T(128)S(6)} %add.116, f32[]{:T(128)S(6)} %add.123), channel_id=1, replica_groups=mesh['dp'=8,'shard'=4] {'shard'}, use_global_device_ids=true, to_apply=%region_19.0 | all-reduce | flops 2 | bytes 16 | tf_op jit(solution)/shard_map/psum | solution.py:56
  537.7 22.3 %all-reduce = (f32[]{:T(128)}, f32[]{:T(128)}) all-reduce(f32[]{:T(128)} %get-tuple-element.10, f32[]{:T(128)} %get-tuple-element.11), channel_id=1, replica_groups=mesh['dp'=8,'shard'=4] {'dp'}, use_global_device_ids=true, to_apply=%region_20.0 | all-reduce | flops 2 | bytes 16 | tf_op jit(solution)/shard_map/psum | solution.py:55
  564.4 14.8 %fusion.4 = (f32[2368,896]{1,0:T(8,128)}, f32[2368,896]{1,0:T(8,128)}) fusion(bf16[2368,896]{1,0:T(8,128)(2,1)} %param.12, f32[]{:T(128)S(6)} %div.21, f32[]{:T(128)S(6)} %div.23, f32[]{:T(128)S(6)} %div.20, f32[2368,896]{1,0:T(8,128)} %get-tuple-element.16, f32[2368,896]{1,0:T(8,128)} %get-tuple-element.17, bf16[2368,896]{1,0:T(8,128)(2,1)} %param.13), kind=kLoop, calls=%fused_computation.18 | loop fusion | flops 36069376 | bytes 42434572 | tf_op jit(solution)/shard_map/add | solution.py:124
  (35 shorter events, 1.0 us)
Async XLA Ops:
  7.2 60.3 %reduce-scatter.10.cloned.1.call-start = ((), (), s32[]{:S(2)}) async-start(), calls=%async_computation.9 | async-start | bytes 757760 | tf_op jit(solution)/shard_map/reduce_scatter | solution.py:31
  44.2 48.5 %reduce-scatter.12.cloned.1.call-start = ((), (), s32[]{:S(2)}) async-start(), calls=%async_computation.10 | async-start | bytes 757760 | tf_op jit(solution)/shard_map/reduce_scatter | solution.py:31
  48.6 103.2 %reduce-scatter.16.cloned.1.call-start = ((), (), s32[]{:S(2)}) async-start(), calls=%async_computation.12 | async-start | bytes 258048 | tf_op jit(solution)/shard_map/reduce_scatter | solution.py:38
  78.7 131.1 %reduce-scatter.14.cloned.1.call-start = ((), (), s32[]{:S(2)}) async-start(), calls=%async_computation.11 | async-start | bytes 258048 | tf_op jit(solution)/shard_map/reduce_scatter | solution.py:38
  92.8 10.8 %slice-start = ((s8[4243456]{0:T(1024)(128)(4,1)}), s8[4194304]{0:T(1024)(128)(4,1)S(1)}, s32[]{:S(2)}) async-start(s8[4243456]{0:T(1024)(128)(4,1)} %bitcast.26), calls=%async_computation.18 | async-start | bytes 8388608
  100.1 3.4 slice-start.1
  103.5 1.8 copy-start.1
  103.5 106.2 %copy-start = (bf16[16,896]{1,0:T(8,128)(2,1)S(1)}, bf16[16,896]{1,0:T(8,128)(2,1)}, u32[]{:S(2)}) copy-start(bf16[16,896]{1,0:T(8,128)(2,1)} %param.8) | copy-start | bytes 86020
  105.2 185.7 %reduce-scatter.20.cloned.1.call-start = ((), (), s32[]{:S(2)}) async-start(), calls=%async_computation.14 | async-start | bytes 757760 | tf_op jit(solution)/shard_map/reduce_scatter | solution.py:31
  245.6 34.4 %slice-start.2 = ((s8[4243456]{0:T(1024)(128)(4,1)}), s8[49152]{0:T(1024)(128)(4,1)S(1)}, s32[]{:S(2)}) async-start(s8[4243456]{0:T(1024)(128)(4,1)} %bitcast.28), calls=%async_computation.20 | async-start | bytes 98304
  245.7 58.1 %reduce-scatter.18.cloned.1.call-start = ((), (), s32[]{:S(2)}) async-start(), calls=%async_computation.13 | async-start | bytes 757760 | tf_op jit(solution)/shard_map/reduce_scatter | solution.py:31
  276.4 3.7 slice-start.3
  282.2 95.6 %reduce-scatter.22.cloned.1.call-start = ((), (), s32[]{:S(2)}) async-start(), calls=%async_computation.15 | async-start | bytes 757760 | tf_op jit(solution)/shard_map/reduce_scatter | solution.py:31
  358.8 92.7 %reduce-scatter.24.cloned.1.call-start = ((), (), s32[]{:S(2)}) async-start(), calls=%async_computation.16 | async-start | bytes 258048 | tf_op jit(solution)/shard_map/reduce_scatter | solution.py:38
  395.5 119.4 %reduce-scatter.26.cloned.1.call-start = ((), (), s32[]{:S(2)}) async-start(), calls=%async_computation.17 | async-start | bytes 757760 | tf_op jit(solution)/shard_map/reduce_scatter | solution.py:31
Sparse Core Ops, SparseCore 0:
  44.4 23.0 reduce-scatter.9
  70.6 22.1 reduce-scatter.11
  96.5 55.2 reduce-scatter.15
  155.4 54.3 reduce-scatter.13
  245.8 21.3 reduce-scatter.19
  282.3 21.3 reduce-scatter.17
  358.9 18.8 reduce-scatter.21
  395.6 55.8 reduce-scatter.23
  493.5 21.3 reduce-scatter.25
